TPU v7x, 256 devices: a whole 4x4x8 slice. The times are simulated.
256 devices in a mesh: row: 8 (over z), col: 32 (over y, x, core).
Axes of the slice: x: 4, y: 4, z: 8, core: 2. Of those that a mesh axis runs over, the one named last changes fastest.
Arguments:
- factor: bfloat16 [131072, 5, 1024], P('col', None, 'row'), may hold values from -0.0625 to 0.0625
- diag_inverse: bfloat16 [5, 1024, 1024], P(None, 'row'), may hold values from -1 to 2
- right_side: float32 [16, 128, 1024], P(None, 'col', 'row'), may hold values from -6 to 6
- tile_order: int32 [128], replicated, may hold values from 0 to 127, each once
- live_segments: int32 [16], replicated, may hold values from 2 to 5
Outputs:
- result: float32 [16, 128, 1024], P(None, 'col', 'row')
Inputs may be any that keep to these rules, and one draw needn't show every extreme that they name: `tile_order`: each of 0 to 127 appears once.
All inputs are finite; a program needn't handle non-finite values.
Results may differ from a plain program's by a relative error of at most 0.0019.
Values may be sent and summed in bfloat16 or wider, within the bound.
A program may use at most 64 MiB of HBM per device.

v0:
```python
import functools
import jax
import jax.numpy as jnp
from jax import lax
from jax.experimental import pallas as pl
from jax.experimental.pallas import tpu as pltpu
from jax.sharding import PartitionSpec as P

MESH = pl.DeviceIdType.MESH
SPARE = 128
NT = (((1,), (1,)), ((), ()))


def encode(value, spare):
    peak = jnp.max(jnp.abs(value), axis=1, keepdims=True)
    power = jnp.ceil(jnp.log2(jnp.maximum(peak, 1e-30)))
    coded = jnp.floor(value * jnp.exp2(14.0 - power) + 0.5)
    powers = jnp.broadcast_to(power, (value.shape[0], spare))
    both = jnp.concatenate([coded, powers], axis=1)
    return both.astype(jnp.int32).astype(jnp.int16)


def decode(coded, count):
    numbers = coded.astype(jnp.int32).astype(jnp.float32)
    scale = jnp.exp2(numbers[:, count:count + 1] - 14.0)
    return numbers[:, :count] * scale


def line_peers(me, count):
    peers = []
    for k in range(count - 1):
        down = count - 1 - k
        down = jnp.where(down <= me, down - 1, down)
        up = jnp.where(me <= k, k + 1, k)
        peers.append(jnp.where(2 * me < count, down, up))
    return peers


def remote(src, dst, send_sem, recv_sem, axis, peer):
    return pltpu.make_async_remote_copy(
        src_ref=src, dst_ref=dst, send_sem=send_sem, recv_sem=recv_sem,
        device_id={axis: peer}, device_id_type=MESH,
    )


def kernel(
    rows, cols, factor_hbm, inverse_hbm, rhs_hbm, order_hbm, live_hbm, out,
    factor, inverse, first, part_out, part_in, sent_all, stored, acc, tail_out, tail_in,
    rhs, order, live,
    factor_sem, inverse_sem, first_sems, part_sems, sent_sems, tail_sems, small_sem,
):
    sections = len(factor)
    rows_dev, tile, width = factor[0].shape
    rhs_count = rhs.shape[0]
    r, c = lax.axis_index("row"), lax.axis_index("col")

    small = (
        pltpu.make_async_copy(rhs_hbm, rhs, small_sem.at[0]),
        pltpu.make_async_copy(order_hbm, order, small_sem.at[1]),
        pltpu.make_async_copy(live_hbm, live, small_sem.at[2]),
    )
    for copy in small:
        copy.start()
    peers = line_peers(r, rows)
    loads = []
    for u in range(sections):
        pair = (
            pltpu.make_async_copy(inverse_hbm.at[u], inverse.at[u], inverse_sem.at[u]),
            pltpu.make_async_copy(factor_hbm.at[u], factor[u], factor_sem.at[u]),
        )
        for copy in pair:
            copy.start()
        loads.append(pair)

    barrier = pltpu.get_barrier_semaphore()
    for axis, me, count in (("row", r, rows), ("col", c, cols)):
        for d in range(1, count):
            pl.semaphore_signal(
                barrier, inc=1, device_id={axis: lax.rem(me + d, count)}, device_id_type=MESH
            )

    for copy in small:
        copy.wait()
    slots = [order[u] for u in range(sections)]
    roots = [lax.div(s, rows_dev) for s in slots]
    locals_ = [lax.rem(s, rows_dev) for s in slots]
    row_ids = lax.broadcasted_iota(jnp.int32, (rhs_count, width), 0)
    limit = jnp.zeros((rhs_count, width), jnp.int32)
    for k in range(rhs_count):
        limit = jnp.where(row_ids == k, live[k], limit)

    def rhs_of(local):
        picked = rhs[:, 0, :]
        for j in range(1, rows_dev):
            picked = jnp.where(local == j, rhs[:, j, :], picked)
        return picked

    for j in range(rows_dev):
        acc[j] = jnp.zeros((rhs_count, tile), jnp.float32)
    first[r] = rhs_of(locals_[0])

    pl.semaphore_wait(barrier, rows - 1 + cols - 1)

    pending = []
    copies = []
    waits = []
    for peer in peers:
        copy = remote(
            first.at[r], first.at[r], first_sems.at[0, peer], first_sems.at[1, r], "row", peer
        )
        copy.start()
        copies.append(copy)
        waits.append(remote(
            first.at[peer], first.at[peer], first_sems.at[0, peer], first_sems.at[1, peer],
            "row", peer,
        ))
    pending += copies

    own = None
    for t in range(sections):
        for copy in waits:
            copy.wait_recv()
        if t == 0:
            remaining = jnp.concatenate([first[s] for s in range(rows)], axis=1)
            kept = first[r]
        else:
            remaining = own
            for peer in peers:
                remaining = remaining + decode(part_in[t, peer], tile)
            kept = remaining[:, :width]
            for s in range(1, rows):
                kept = jnp.where(r == s, remaining[:, s * width:(s + 1) * width], kept)
        high = remaining.astype(jnp.bfloat16)
        rest = remaining - high.astype(jnp.float32)
        middle = rest.astype(jnp.bfloat16)
        low = (rest - middle.astype(jnp.float32)).astype(jnp.bfloat16)
        loads[t][0].wait()
        parts = lax.dot_general(
            jnp.concatenate([high, middle, low], axis=0), inverse[t], NT,
            preferred_element_type=jnp.float32,
        )
        solved = (
            parts[2 * rhs_count:] + parts[rhs_count:2 * rhs_count]
        ) + parts[:rhs_count]
        is_live = limit > t
        sent_all[t][c] = jnp.where(is_live, solved, 0.0).astype(jnp.bfloat16)
        sends = []
        for d in range(1, cols):
            copy = remote(
                sent_all[t].at[c], sent_all[t].at[c], sent_sems.at[0, t, d],
                sent_sems.at[1, t, d], "col", lax.rem(c + d, cols),
            )
            copy.start()
            sends.append(copy)
        pending += sends
        stored[t] = jnp.where(is_live, solved, kept)
        if t + 1 < sections:
            local = locals_[t + 1]
            mine = rhs_of(local)
            base = jnp.concatenate(
                [jnp.where(r == s, mine, 0.0) for s in range(rows)], axis=1
            ) - acc[local]
        loads[t][1].wait()
        for copy in sends:
            copy.wait_recv()
        sent = sent_all[t][roots[t]]
        if t + 1 < sections:
            own = base - lax.dot_general(
                sent, factor[t][local], NT, preferred_element_type=jnp.float32
            )
            part_out[t + 1] = encode(own, SPARE)
            copies, waits = [], []
            for peer in peers:
                copy = remote(
                    part_out.at[t + 1], part_in.at[t + 1, r], part_sems.at[0, t + 1, peer],
                    part_sems.at[1, t + 1, r], "row", peer,
                )
                copy.start()
                copies.append(copy)
                waits.append(remote(
                    part_out.at[t + 1], part_in.at[t + 1, peer], part_sems.at[0, t + 1, peer],
                    part_sems.at[1, t + 1, peer], "row", peer,
                ))
            pending += copies
            for j in range(rows_dev):
                acc[j] += lax.dot_general(
                    sent, factor[t][j], NT, preferred_element_type=jnp.float32
                )
        else:
            totals = [
                acc[j] + lax.dot_general(
                    sent, factor[t][j], NT, preferred_element_type=jnp.float32
                )
                for j in range(rows_dev)
            ]

    spans = []
    for s in range(rows):
        spans.append([x[:, s * width:(s + 1) * width] for x in totals])
        tail_out[s] = encode(jnp.concatenate(spans[s], axis=1), SPARE)
    tails = []
    for peer in peers:
        copy = remote(
            tail_out.at[peer], tail_in.at[r], tail_sems.at[0, peer], tail_sems.at[1, r], "row", peer
        )
        copy.start()
        tails.append(copy)
    pending += tails
    values = []
    for j in range(rows_dev):
        total = spans[0][j]
        for s in range(1, rows):
            total = jnp.where(r == s, spans[s][j], total)
        values.append(rhs[:, j, :] - total)
    others = []
    for peer in peers:
        remote(
            tail_out.at[peer], tail_in.at[peer], tail_sems.at[0, peer], tail_sems.at[1, peer],
            "row", peer,
        ).wait_recv()
        others.append(decode(tail_in[peer], rows_dev * width))
    for j in range(rows_dev):
        value = values[j]
        for other in others:
            value = value - other[:, j * width:(j + 1) * width]
        for t in range(sections):
            value = jnp.where(slots[t] == c * rows_dev + j, stored[t], value)
        out[:, j, :] = value
    for copy in pending:
        copy.wait_send()


def per_device(rows, cols, factor, diag_inverse, right_side, tile_order, live_segments):
    sections, width, tile = diag_inverse.shape
    rhs_count, rows_dev, _ = right_side.shape
    panel = jnp.transpose(factor, (1, 0, 2)).reshape(sections, rows_dev, tile, width)
    vmem = pl.BlockSpec(memory_space=pltpu.VMEM)
    hbm = pl.BlockSpec(memory_space=pl.ANY)
    f32, bf16, i16 = jnp.float32, jnp.bfloat16, jnp.int16
    return pl.pallas_call(
        functools.partial(kernel, rows, cols),
        out_shape=jax.ShapeDtypeStruct(right_side.shape, f32),
        in_specs=[hbm] * 5,
        out_specs=vmem,
        scratch_shapes=[
            [pltpu.VMEM((rows_dev, tile, width), bf16)] * sections,
            pltpu.VMEM((sections, width, tile), bf16),
            pltpu.VMEM((rows, rhs_count, width), f32),
            pltpu.VMEM((sections, rhs_count, tile + SPARE), i16),
            pltpu.VMEM((sections, rows, rhs_count, tile + SPARE), i16),
            [pltpu.VMEM((cols, rhs_count, width), bf16)] * sections,
            pltpu.VMEM((sections, rhs_count, width), f32),
            pltpu.VMEM((rows_dev, rhs_count, tile), f32),
            pltpu.VMEM((rows, rhs_count, rows_dev * width + SPARE), i16),
            pltpu.VMEM((rows, rhs_count, rows_dev * width + SPARE), i16),
            pltpu.VMEM(right_side.shape, f32),
            pltpu.SMEM(tile_order.shape, jnp.int32),
            pltpu.SMEM(live_segments.shape, jnp.int32),
            pltpu.SemaphoreType.DMA((sections,)),
            pltpu.SemaphoreType.DMA((sections,)),
            pltpu.SemaphoreType.DMA((2, rows)),
            pltpu.SemaphoreType.DMA((2, sections, rows)),
            pltpu.SemaphoreType.DMA((2, sections, cols)),
            pltpu.SemaphoreType.DMA((2, rows)),
            pltpu.SemaphoreType.DMA((3,)),
        ],
        compiler_params=pltpu.CompilerParams(
            collective_id=0, has_side_effects=True, vmem_limit_bytes=67043328
        ),
    )(panel, diag_inverse, right_side, tile_order, live_segments)


def solution(mesh):
    return jax.shard_map(
        functools.partial(per_device, mesh.shape["row"], mesh.shape["col"]),
        mesh=mesh,
        in_specs=(P("col", None, "row"), P(None, "row", None), P(None, "col", "row"), P(), P()),
        out_specs=P(None, "col", "row"),
        check_vma=False,
    )
```

profile of v0, /device:TPU:1, one launch (start us, length us, event | category | flops | bytes accessed | tf_op | source)
XLA Modules:
  0.0 92.4 jit_solution(6527593986366457381)
XLA Ops:
  0.0 91.0 %shard_map.55 = f32[16,4,128]{2,1,0:T(4,128)} custom-call(bf16[5,4,1024,128]{3,2,1,0:T(8,128)(2,1)} %bitcast.3, bf16[5,128,1024]{2,1,0:T(8,128)(2,1)} %inverse_hbm.1, f32[16,4,128]{2,1,0:T(4,128)} %rhs_hbm.1, s32[128]{0:T(128)} %order_hbm.1, s32[16]{0:T(128)} %live_hbm.1), custom_call_target="tpu_custom_call" | custom-call | tf_op jit(solution)/shard_map/pallas_call | solution.py:240
  91.0 1.4 %copy.7 = f32[16,4,128]{2,1,0:T(4,128)} copy(f32[16,4,128]{2,1,0:T(4,128)} %shard_map.55) | data formatting | bytes 65536
where the time goes:
time: 92.5 us; the launch traced here: 92.4 us
  Pallas kernels  91 us (98%)
  local copies, waits for them, and re-layouts  1.38 us (1%)
    pallas_call x1, Pallas kernels, per_device(): pl.pallas_call(functools.partial(kernel, rows, cols), out_shape=jax.Shape...  91 us

commit v1 on v0

v1 whole, which is shorter than its diff:
```python
import functools
import jax
import jax.numpy as jnp
from jax import lax
from jax.experimental import pallas as pl
from jax.experimental.pallas import tpu as pltpu
from jax.sharding import PartitionSpec as P

MESH = pl.DeviceIdType.MESH
SPARE = 128
DEPTH = 3
NT = (((1,), (1,)), ((), ()))


def encode(value, spare):
    peak = jnp.max(jnp.abs(value), axis=1, keepdims=True)
    power = jnp.ceil(jnp.log2(jnp.maximum(peak, 1e-30)))
    coded = jnp.floor(value * jnp.exp2(14.0 - power) + 0.5)
    powers = jnp.broadcast_to(power, (value.shape[0], spare))
    both = jnp.concatenate([coded, powers], axis=1)
    return both.astype(jnp.int32).astype(jnp.int16)


def decode(coded, count):
    numbers = coded.astype(jnp.int32).astype(jnp.float32)
    scale = jnp.exp2(numbers[:, count:count + 1] - 14.0)
    return numbers[:, :count] * scale


def ring_order(count):
    return sorted(range(1, count), key=lambda d: -min(d, count - d))


def remote(src, dst, send_sem, recv_sem, device):
    return pltpu.make_async_remote_copy(
        src_ref=src, dst_ref=dst, send_sem=send_sem, recv_sem=recv_sem,
        device_id=device, device_id_type=MESH,
    )


def dot_nt(a, b):
    return lax.dot_general(a, b, NT, preferred_element_type=jnp.float32)


def kernel(
    rows, cols, blocks, factor_hbm, inverse_hbm, rhs_hbm, order_hbm, live_hbm, out,
    factor, inverse, cand, theirs, pieces, mine, panels,
    b_own, b_pair, b_chip, b0_in, b1_in, b0_all, b1_all,
    part_out, part_in, stored, acc, tail_out, tail_in, rhs, order, live,
    factor_sem, inverse_sem, small_sem, pair_sems, b_sems, piece_sems, panel_sems,
    b0_sems, b1_sems, part_sems, stored_sems, tail_sems,
):
    sections = len(factor)
    rows_dev, tile, width = factor[0].shape
    rhs_count = rhs.shape[0]
    chips = cols // 2
    piece = tile // chips
    r, c = lax.axis_index("row"), lax.axis_index("col")
    chip, core = lax.div(c, 2), lax.rem(c, 2)
    index = {tu: i for i, tu in enumerate(blocks)}

    small = (
        pltpu.make_async_copy(rhs_hbm, rhs, small_sem.at[0]),
        pltpu.make_async_copy(order_hbm, order, small_sem.at[1]),
        pltpu.make_async_copy(live_hbm, live, small_sem.at[2]),
    )
    for copy in small:
        copy.start()
    factor_loads = []
    for u in range(sections):
        copy = pltpu.make_async_copy(factor_hbm.at[u], factor[u], factor_sem.at[u])
        copy.start()
        factor_loads.append(copy)
    inverse_load = pltpu.make_async_copy(inverse_hbm, inverse, inverse_sem.at[0])
    inverse_load.start()

    barrier = pltpu.get_barrier_semaphore()
    for axis, me, count in (("row", r, rows), ("col", c, cols)):
        for d in range(1, count):
            pl.semaphore_signal(
                barrier, inc=1, device_id={axis: lax.rem(me + d, count)}, device_id_type=MESH
            )

    for copy in small:
        copy.wait()
    slots = [order[u] for u in range(sections)]
    locals_ = [lax.rem(s, rows_dev) for s in slots]
    root_core = [lax.rem(lax.div(s, rows_dev), 2) for s in slots]
    root_chip = [lax.div(s, 2 * rows_dev) for s in slots]
    row_ids = lax.broadcasted_iota(jnp.int32, (rhs_count, width), 0)
    limit = jnp.zeros((rhs_count, width), jnp.int32)
    for k in range(rhs_count):
        limit = jnp.where(row_ids == k, live[k], limit)

    for t in range(sections):
        picked = rhs[:, 0, :]
        for j in range(1, rows_dev):
            picked = jnp.where(locals_[t] == j, rhs[:, j, :], picked)
        b_own[t] = picked
    for copy in factor_loads + [inverse_load]:
        copy.wait()

    peers = [lax.rem(r + d, rows) for d in ring_order(rows)]
    others = [lax.rem(chip + d, chips) for d in range(1, chips)]

    def trail(t, sent):
        for j in range(rows_dev):
            update = dot_nt(sent, factor[t][j])
            if t == 0:
                acc[j] = update
            else:
                acc[j] += update

    @pl.when(core == 0)
    def _():
        pl.semaphore_wait(barrier, rows - 1 + cols - 1)
        pair = remote(b_own, b_pair, b_sems.at[0], b_sems.at[1], {"col": c + 1})
        pair.start()

        def scatter(i):
            t, u = blocks[i]
            remote(
                theirs[i], theirs[i], pair_sems.at[0, i], pair_sems.at[1, i], {"col": c + 1}
            ).wait_recv()
            for s in range(0, tile, 256):
                own = factor[u][locals_[t], pl.ds(s, 256), :]
                cand[i][s:s + 256] = jnp.where(
                    root_core[t] == 1, theirs[i][s:s + 256], own
                )
            for p in others:
                remote(
                    cand[i].at[pl.ds(pl.multiple_of(p * piece, piece), piece)],
                    pieces[i].at[chip], piece_sems.at[0, i], piece_sems.at[1, i],
                    {"col": 2 * p},
                ).start()
            pieces[i][chip] = cand[i][pl.ds(pl.multiple_of(chip * piece, piece), piece)]

        def gather(i):
            t, u = blocks[i]
            some = pieces[i].at[pl.ds(0, chips - 1)]
            remote(some, some, piece_sems.at[0, i], piece_sems.at[1, i], {"col": c + 1}).wait_recv()
            mine[i] = pieces[i][root_chip[t]]
            here = pl.ds(pl.multiple_of(chip * piece, piece), piece)
            for p in [chip] + others:
                remote(
                    mine.at[i], panels[i].at[here], panel_sems.at[0, i], panel_sems.at[1, i],
                    {"col": 2 * p + 1},
                ).start()

        for i in range(min(DEPTH, len(blocks))):
            scatter(i)
        for i in range(len(blocks)):
            gather(i)
            if i + DEPTH < len(blocks):
                scatter(i + DEPTH)

        for t in range(sections):
            remote(
                stored.at[t], stored.at[t], stored_sems.at[0, t], stored_sems.at[1, t],
                {"col": c + 1},
            ).wait_recv()
            trail(t, jnp.where(limit > t, stored[t], 0.0).astype(jnp.bfloat16))

        pair.wait_send()
        for i in range(len(blocks)):
            some = pieces[i].at[pl.ds(0, chips - 1)]
            remote(some, some, piece_sems.at[0, i], piece_sems.at[1, i], {"col": c + 1}).wait_send()
            remote(
                panels[i], panels[i], panel_sems.at[0, i], panel_sems.at[1, i], {"col": c + 1}
            ).wait_send()

    @pl.when(core == 1)
    def _():
        for i, (t, u) in enumerate(blocks):
            for s in range(0, tile, 256):
                cand[i][s:s + 256] = factor[u][locals_[t], pl.ds(s, 256), :]
        pl.semaphore_wait(barrier, rows - 1 + cols - 1)
        remote(b_own, b_pair, b_sems.at[0], b_sems.at[1], {"col": c - 1}).wait_recv()
        for t in range(sections):
            b_chip[t] = jnp.where(root_core[t] == 1, b_own[t], b_pair[t])
        for p in others:
            remote(
                b_chip.at[0], b0_in.at[chip], b0_sems.at[0, 0], b0_sems.at[1, 0],
                {"col": 2 * p + 1},
            ).start()
        pairs = []
        for i in range(len(blocks)):
            copy = remote(
                cand[i], theirs[i], pair_sems.at[0, i], pair_sems.at[1, i], {"col": c - 1}
            )
            copy.start()
            pairs.append(copy)
        later = b_chip.at[pl.ds(1, sections - 1)]
        for p in others:
            remote(
                later, b1_in.at[chip], b1_sems.at[0, 0], b1_sems.at[1, 0], {"col": 2 * p + 1}
            ).start()
        b0_in[chip] = b_chip[0]
        b1_in[chip] = b_chip[1:]

        some = b0_in.at[pl.ds(0, chips - 1)]
        b0_wait = remote(some, some, b0_sems.at[0, 0], b0_sems.at[1, 0], {"col": c - 1})
        b0_wait.wait_recv()
        b0_all[r] = b0_in[root_chip[0]]
        for peer in peers:
            remote(
                b0_all.at[r], b0_all.at[r], b0_sems.at[0, 1], b0_sems.at[1, 1], {"row": peer}
            ).start()
        some = b1_in.at[pl.ds(0, chips - 1)]
        b1_wait = remote(some, some, b1_sems.at[0, 0], b1_sems.at[1, 0], {"col": c - 1})
        b1_wait.wait_recv()
        for t in range(1, sections):
            b1_all[r, t - 1] = b1_in[root_chip[t], t - 1]
        for peer in peers:
            remote(
                b1_all.at[r], b1_all.at[r], b1_sems.at[0, 1], b1_sems.at[1, 1], {"row": peer}
            ).start()
        some = b0_all.at[pl.ds(0, rows - 1)]
        b0_row = remote(some, some, b0_sems.at[0, 1], b0_sems.at[1, 1], {"col": c - 1})
        some = b1_all.at[pl.ds(0, rows - 1)]
        b1_row = remote(some, some, b1_sems.at[0, 1], b1_sems.at[1, 1], {"col": c - 1})

        def panel(t, u):
            i = index[t, u]
            remote(
                panels[i], panels[i], panel_sems.at[0, i], panel_sems.at[1, i], {"col": c - 1}
            ).wait_recv()
            return panels[i][...]

        sents, pending = [], []
        own, older = None, None
        for t in range(sections):
            if t == 0:
                b0_row.wait_recv()
                remaining = jnp.concatenate([b0_all[s] for s in range(rows)], axis=1)
            else:
                remaining = jnp.concatenate(
                    [b1_all[s, t - 1] for s in range(rows)], axis=1
                ) - own
                for peer in reversed(peers):
                    remote(
                        part_out.at[t], part_in.at[t, peer], part_sems.at[0, t, peer],
                        part_sems.at[1, t, peer], {"row": peer},
                    ).wait_recv()
                    remaining = remaining - decode(part_in[t, peer], tile)
            kept = remaining[:, :width]
            for s in range(1, rows):
                kept = jnp.where(r == s, remaining[:, s * width:(s + 1) * width], kept)
            high = remaining.astype(jnp.bfloat16)
            rest = remaining - high.astype(jnp.float32)
            middle = rest.astype(jnp.bfloat16)
            low = (rest - middle.astype(jnp.float32)).astype(jnp.bfloat16)
            parts = dot_nt(jnp.concatenate([high, middle, low], axis=0), inverse[t])
            solved = (
                parts[2 * rhs_count:] + parts[rhs_count:2 * rhs_count]
            ) + parts[:rhs_count]
            is_live = limit > t
            sent = jnp.where(is_live, solved, 0.0).astype(jnp.bfloat16)
            sents.append(sent)
            if t + 1 < sections:
                own = dot_nt(sent, panel(t + 1, t))
                if older is not None:
                    own = own + older
                part_out[t + 1] = encode(own, SPARE)
                for peer in peers:
                    copy = remote(
                        part_out.at[t + 1], part_in.at[t + 1, r], part_sems.at[0, t + 1, peer],
                        part_sems.at[1, t + 1, r], {"row": peer},
                    )
                    copy.start()
                    pending.append(copy)
            stored[t] = jnp.where(is_live, solved, kept)
            copy = remote(
                stored.at[t], stored.at[t], stored_sems.at[0, t], stored_sems.at[1, t],
                {"col": c - 1},
            )
            copy.start()
            pending.append(copy)
            trail(t, sent)
            if t == 0:
                b1_row.wait_recv()
            if t + 2 < sections:
                older = dot_nt(sents[0], panel(t + 2, 0))
                for u in range(1, t + 1):
                    older = older + dot_nt(sents[u], panel(t + 2, u))

        for wait in (b0_wait, b1_wait, b0_row, b1_row):
            wait.wait_send()
        for copy in pairs + pending:
            copy.wait_send()

    spans = []
    totals = [acc[j] for j in range(rows_dev)]
    for s in range(rows):
        spans.append([x[:, s * width:(s + 1) * width] for x in totals])
        tail_out[s] = encode(jnp.concatenate(spans[s], axis=1), SPARE)
    tails = []
    for peer in peers:
        copy = remote(
            tail_out.at[peer], tail_in.at[r], tail_sems.at[0, peer], tail_sems.at[1, r],
            {"row": peer},
        )
        copy.start()
        tails.append(copy)
    values = []
    for j in range(rows_dev):
        total = spans[0][j]
        for s in range(1, rows):
            total = jnp.where(r == s, spans[s][j], total)
        values.append(rhs[:, j, :] - total)
    for peer in reversed(peers):
        remote(
            tail_out.at[peer], tail_in.at[peer], tail_sems.at[0, peer], tail_sems.at[1, peer],
            {"row": peer},
        ).wait_recv()
        other = decode(tail_in[peer], rows_dev * width)
        for j in range(rows_dev):
            values[j] = values[j] - other[:, j * width:(j + 1) * width]
    for j in range(rows_dev):
        value = values[j]
        for t in range(sections):
            value = jnp.where(slots[t] == c * rows_dev + j, stored[t], value)
        out[:, j, :] = value
    for copy in tails:
        copy.wait_send()


def per_device(rows, cols, factor, diag_inverse, right_side, tile_order, live_segments):
    sections, width, tile = diag_inverse.shape
    rhs_count, rows_dev, _ = right_side.shape
    panel = jnp.transpose(factor, (1, 0, 2)).reshape(sections, rows_dev, tile, width)
    blocks = [(t, u) for t in range(1, sections) for u in range(t)]
    count, chips = len(blocks), cols // 2
    vmem = pl.BlockSpec(memory_space=pltpu.VMEM)
    hbm = pl.BlockSpec(memory_space=pl.ANY)
    f32, bf16, i16 = jnp.float32, jnp.bfloat16, jnp.int16
    dma = pltpu.SemaphoreType.DMA
    return pl.pallas_call(
        functools.partial(kernel, rows, cols, blocks),
        out_shape=jax.ShapeDtypeStruct(right_side.shape, f32),
        in_specs=[hbm] * 5,
        out_specs=vmem,
        scratch_shapes=[
            [pltpu.VMEM((rows_dev, tile, width), bf16)] * sections,
            pltpu.VMEM((sections, width, tile), bf16),
            [pltpu.VMEM((tile, width), bf16)] * count,
            [pltpu.VMEM((tile, width), bf16)] * count,
            [pltpu.VMEM((chips, tile // chips, width), bf16)] * count,
            pltpu.VMEM((count, tile // chips, width), bf16),
            [pltpu.VMEM((tile, width), bf16)] * count,
            pltpu.VMEM((sections, rhs_count, width), f32),
            pltpu.VMEM((sections, rhs_count, width), f32),
            pltpu.VMEM((sections, rhs_count, width), f32),
            pltpu.VMEM((chips, rhs_count, width), f32),
            pltpu.VMEM((chips, sections - 1, rhs_count, width), f32),
            pltpu.VMEM((rows, rhs_count, width), f32),
            pltpu.VMEM((rows, sections - 1, rhs_count, width), f32),
            pltpu.VMEM((sections, rhs_count, tile + SPARE), i16),
            pltpu.VMEM((sections, rows, rhs_count, tile + SPARE), i16),
            pltpu.VMEM((sections, rhs_count, width), f32),
            pltpu.VMEM((rows_dev, rhs_count, tile), f32),
            pltpu.VMEM((rows, rhs_count, rows_dev * width + SPARE), i16),
            pltpu.VMEM((rows, rhs_count, rows_dev * width + SPARE), i16),
            pltpu.VMEM(right_side.shape, f32),
            pltpu.SMEM(tile_order.shape, jnp.int32),
            pltpu.SMEM(live_segments.shape, jnp.int32),
            dma((sections,)),
            dma((1,)),
            dma((3,)),
            dma((2, count)),
            dma((2,)),
            dma((2, count)),
            dma((2, count)),
            dma((2, 2)),
            dma((2, 2)),
            dma((2, sections, rows)),
            dma((2, sections)),
            dma((2, rows)),
        ],
        compiler_params=pltpu.CompilerParams(
            collective_id=0, has_side_effects=True, vmem_limit_bytes=67043328
        ),
    )(panel, diag_inverse, right_side, tile_order, live_segments)


def solution(mesh):
    return jax.shard_map(
        functools.partial(per_device, mesh.shape["row"], mesh.shape["col"]),
        mesh=mesh,
        in_specs=(P("col", None, "row"), P(None, "row", None), P(None, "col", "row"), P(), P()),
        out_specs=P(None, "col", "row"),
        check_vma=False,
    )
```

time: 92.5 us -> 65.6 us (0.71)
  Pallas kernels: 91 us -> 64.1 us
    pallas_call x1, Pallas kernels: 91 us -> 64.1 us  [per_device(): pl.pallas_call(functools.partial(kernel, rows, cols, blocks), out_shape=j...]
where the time goes in v1:
time: 65.6 us; the launch traced here: 65.5 us
  Pallas kernels  64.1 us (98%)
  local copies, waits for them, and re-layouts  1.38 us (2%)
    pallas_call x1, Pallas kernels, per_device(): pl.pallas_call(functools.partial(kernel, rows, cols, blocks), out_shape=j...  64.1 us
    unnamed x1, local copies, waits for them, and re-layouts  1.38 us

profile of v1, /device:TPU:1, one launch (start us, length us, event | category | flops | bytes accessed | tf_op | source)
XLA Modules:
  0.0 65.5 jit_solution(747923396698876598)
XLA Ops:
  0.0 64.1 %shard_map.55 = f32[16,4,128]{2,1,0:T(4,128)} custom-call(bf16[5,4,1024,128]{3,2,1,0:T(8,128)(2,1)} %bitcast.3, bf16[5,128,1024]{2,1,0:T(8,128)(2,1)} %inverse_hbm.1, f32[16,4,128]{2,1,0:T(4,128)} %rhs_hbm.1, s32[128]{0:T(128)} %order_hbm.1, s32[16]{0:T(128)} %live_hbm.1), custom_call_target="tpu_custom_call" | custom-call | tf_op jit(solution)/shard_map/pallas_call | solution.py:338
  64.1 1.4 %copy.7 = f32[16,4,128]{2,1,0:T(4,128)} copy(f32[16,4,128]{2,1,0:T(4,128)} %shard_map.55) | data formatting | bytes 65536

commit v2 on v1

--- a/solution.py
+++ b/solution.py
@@ -8,7 +8,9 @@
 
 MESH = pl.DeviceIdType.MESH
 SPARE = 128
-DEPTH = 3
+SIDE = 4
+DIRECT = 10
+ORDER = "s0 s1 s2 s3 g0 s4 g1 s5 g2 s6 g3 s7 g4 s8 g5 s9 g6 g7 g8 g9"
 NT = (((1,), (1,)), ((), ()))
 
 
@@ -44,10 +46,10 @@
 
 def kernel(
     rows, cols, blocks, factor_hbm, inverse_hbm, rhs_hbm, order_hbm, live_hbm, out,
-    factor, inverse, cand, theirs, pieces, mine, panels,
-    b_own, b_pair, b_chip, b0_in, b1_in, b0_all, b1_all,
+    factor, inverse, cand, theirs, pieces, mine, panels, quarters, quarter, sixteenths, joined,
+    b_own, b_pair, b_chip, b0_in, b0_all, b_line, b_turn, b_cross,
     part_out, part_in, stored, acc, tail_out, tail_in, rhs, order, live,
-    factor_sem, inverse_sem, small_sem, pair_sems, b_sems, piece_sems, panel_sems,
+    factor_sem, inverse_sem, small_sem, pair_sems, b_sems, piece_sems, panel_sems, line_sems,
     b0_sems, b1_sems, part_sems, stored_sems, tail_sems,
 ):
     sections = len(factor)
@@ -117,7 +119,7 @@
         pair = remote(b_own, b_pair, b_sems.at[0], b_sems.at[1], {"col": c + 1})
         pair.start()
 
-        def scatter(i):
+        def merge(i):
             t, u = blocks[i]
             remote(
                 theirs[i], theirs[i], pair_sems.at[0, i], pair_sems.at[1, i], {"col": c + 1}
@@ -127,32 +129,97 @@
                 cand[i][s:s + 256] = jnp.where(
                     root_core[t] == 1, theirs[i][s:s + 256], own
                 )
+
+        def span(index, size):
+            return pl.ds(pl.multiple_of(index * size, size), size)
+
+        def scatter(i):
+            merge(i)
             for p in others:
                 remote(
-                    cand[i].at[pl.ds(pl.multiple_of(p * piece, piece), piece)],
-                    pieces[i].at[chip], piece_sems.at[0, i], piece_sems.at[1, i],
-                    {"col": 2 * p},
-                ).start()
-            pieces[i][chip] = cand[i][pl.ds(pl.multiple_of(chip * piece, piece), piece)]
+                    cand[i].at[span(p, piece)], pieces[i].at[chip],
+                    piece_sems.at[0, i], piece_sems.at[1, i], {"col": 2 * p},
+                ).start()
+            pieces[i][chip] = cand[i][span(chip, piece)]
 
         def gather(i):
             t, u = blocks[i]
             some = pieces[i].at[pl.ds(0, chips - 1)]
             remote(some, some, piece_sems.at[0, i], piece_sems.at[1, i], {"col": c + 1}).wait_recv()
             mine[i] = pieces[i][root_chip[t]]
-            here = pl.ds(pl.multiple_of(chip * piece, piece), piece)
             for p in [chip] + others:
                 remote(
-                    mine.at[i], panels[i].at[here], panel_sems.at[0, i], panel_sems.at[1, i],
-                    {"col": 2 * p + 1},
-                ).start()
-
-        for i in range(min(DEPTH, len(blocks))):
-            scatter(i)
-        for i in range(len(blocks)):
-            gather(i)
-            if i + DEPTH < len(blocks):
-                scatter(i + DEPTH)
+                    mine.at[i], panels[i].at[span(chip, piece)],
+                    panel_sems.at[0, i], panel_sems.at[1, i], {"col": 2 * p + 1},
+                ).start()
+
+        part = tile // SIDE
+        ahead = [d for d in ring_order(SIDE)]
+
+        def place(i):
+            t, u = blocks[i]
+            here = (lax.rem(chip, SIDE), lax.div(chip, SIDE))
+            root = (lax.rem(root_chip[t], SIDE), lax.div(root_chip[t], SIDE))
+            if i % 2:
+                here, root = here[::-1], root[::-1]
+                return here, root, lambda a, b: 2 * (a * SIDE + b)
+            return here, root, lambda a, b: 2 * (b * SIDE + a)
+
+        def line(i, stage, some):
+            return remote(
+                some, some, line_sems.at[stage, 0, i], line_sems.at[stage, 1, i], {"col": c + 1}
+            )
+
+        def first_line(i):
+            merge(i)
+            (a, b), root, core_of = place(i)
+            for d in ahead:
+                to = lax.rem(a + d, SIDE)
+                remote(
+                    cand[i].at[span(to, part)], quarters[i].at[a],
+                    line_sems.at[0, 0, i], line_sems.at[0, 1, i], {"col": core_of(to, b)},
+                ).start()
+            quarters[i][a] = cand[i][span(a, part)]
+
+        def second_line(i):
+            (a, b), root, core_of = place(i)
+            line(i, 0, quarters[i].at[pl.ds(0, SIDE - 1)]).wait_recv()
+            quarter[i][...] = quarters[i][root[0]]
+            for d in ahead:
+                to = lax.rem(b + d, SIDE)
+                remote(
+                    quarter[i].at[span(to, piece)], sixteenths[i].at[b],
+                    line_sems.at[1, 0, i], line_sems.at[1, 1, i], {"col": core_of(a, to)},
+                ).start()
+            sixteenths[i][b] = quarter[i][span(b, piece)]
+
+        def third_line(i):
+            (a, b), root, core_of = place(i)
+            line(i, 1, sixteenths[i].at[pl.ds(0, SIDE - 1)]).wait_recv()
+            joined[i][span(b, piece)] = sixteenths[i][root[1]]
+            for d in ahead:
+                remote(
+                    joined[i].at[span(b, piece)], joined[i].at[span(b, piece)],
+                    line_sems.at[2, 0, i], line_sems.at[2, 1, i],
+                    {"col": core_of(a, lax.rem(b + d, SIDE))},
+                ).start()
+
+        def fourth_line(i):
+            (a, b), root, core_of = place(i)
+            line(i, 2, joined[i].at[pl.ds(0, part - piece)]).wait_recv()
+            for d in ahead + [0]:
+                remote(
+                    joined[i], panels[i].at[span(a, part)],
+                    panel_sems.at[0, i], panel_sems.at[1, i],
+                    {"col": core_of(lax.rem(a + d, SIDE), b) + 1},
+                ).start()
+
+        direct = range(DIRECT)
+        run = dict(
+            s=scatter, g=gather, a=first_line, b=second_line, c=third_line, d=fourth_line
+        )
+        for op in ORDER.split():
+            run[op[0]](int(op[1:]))
 
         for t in range(sections):
             remote(
@@ -163,8 +230,15 @@
 
         pair.wait_send()
         for i in range(len(blocks)):
-            some = pieces[i].at[pl.ds(0, chips - 1)]
-            remote(some, some, piece_sems.at[0, i], piece_sems.at[1, i], {"col": c + 1}).wait_send()
+            if i in direct:
+                some = pieces[i].at[pl.ds(0, chips - 1)]
+                remote(
+                    some, some, piece_sems.at[0, i], piece_sems.at[1, i], {"col": c + 1}
+                ).wait_send()
+            else:
+                line(i, 0, quarters[i].at[pl.ds(0, SIDE - 1)]).wait_send()
+                line(i, 1, sixteenths[i].at[pl.ds(0, SIDE - 1)]).wait_send()
+                line(i, 2, joined[i].at[pl.ds(0, part - piece)]).wait_send()
             remote(
                 panels[i], panels[i], panel_sems.at[0, i], panel_sems.at[1, i], {"col": c + 1}
             ).wait_send()
@@ -183,6 +257,13 @@
                 b_chip.at[0], b0_in.at[chip], b0_sems.at[0, 0], b0_sems.at[1, 0],
                 {"col": 2 * p + 1},
             ).start()
+        chip_y, chip_x = lax.div(chip, SIDE), lax.rem(chip, SIDE)
+        for d in ring_order(SIDE):
+            to = chip_y * SIDE + lax.rem(chip_x + d, SIDE)
+            remote(
+                b_chip.at[pl.ds(1, sections - 1)], b_line.at[chip_x],
+                b1_sems.at[0, 0], b1_sems.at[1, 0], {"col": 2 * to + 1},
+            ).start()
         pairs = []
         for i in range(len(blocks)):
             copy = remote(
@@ -190,13 +271,8 @@
             )
             copy.start()
             pairs.append(copy)
-        later = b_chip.at[pl.ds(1, sections - 1)]
-        for p in others:
-            remote(
-                later, b1_in.at[chip], b1_sems.at[0, 0], b1_sems.at[1, 0], {"col": 2 * p + 1}
-            ).start()
         b0_in[chip] = b_chip[0]
-        b1_in[chip] = b_chip[1:]
+        b_line[chip_x] = b_chip[1:]
 
         some = b0_in.at[pl.ds(0, chips - 1)]
         b0_wait = remote(some, some, b0_sems.at[0, 0], b0_sems.at[1, 0], {"col": c - 1})
@@ -206,19 +282,27 @@
             remote(
                 b0_all.at[r], b0_all.at[r], b0_sems.at[0, 1], b0_sems.at[1, 1], {"row": peer}
             ).start()
-        some = b1_in.at[pl.ds(0, chips - 1)]
-        b1_wait = remote(some, some, b1_sems.at[0, 0], b1_sems.at[1, 0], {"col": c - 1})
-        b1_wait.wait_recv()
+        some = b_line.at[pl.ds(0, SIDE - 1)]
+        line_wait = remote(some, some, b1_sems.at[0, 0], b1_sems.at[1, 0], {"col": c - 1})
+        line_wait.wait_recv()
         for t in range(1, sections):
-            b1_all[r, t - 1] = b1_in[root_chip[t], t - 1]
-        for peer in peers:
-            remote(
-                b1_all.at[r], b1_all.at[r], b1_sems.at[0, 1], b1_sems.at[1, 1], {"row": peer}
+            b_turn[t - 1] = b_line[lax.rem(root_chip[t], SIDE), t - 1]
+        for d in ring_order(SIDE):
+            to = lax.rem(chip_y + d, SIDE) * SIDE + chip_x
+            remote(
+                b_turn, b_cross.at[chip_y], b1_sems.at[0, 1], b1_sems.at[1, 1],
+                {"col": 2 * to + 1},
             ).start()
+        b_cross[chip_y] = b_turn[...]
+        some = b_cross.at[pl.ds(0, SIDE - 1)]
+        cross_wait = remote(some, some, b1_sems.at[0, 1], b1_sems.at[1, 1], {"col": c - 1})
+
+        def placed(t):
+            value = b_cross[lax.div(root_chip[t], SIDE), t - 1]
+            return jnp.concatenate([jnp.where(r == s, value, 0.0) for s in range(rows)], axis=1)
+
         some = b0_all.at[pl.ds(0, rows - 1)]
         b0_row = remote(some, some, b0_sems.at[0, 1], b0_sems.at[1, 1], {"col": c - 1})
-        some = b1_all.at[pl.ds(0, rows - 1)]
-        b1_row = remote(some, some, b1_sems.at[0, 1], b1_sems.at[1, 1], {"col": c - 1})
 
         def panel(t, u):
             i = index[t, u]
@@ -234,9 +318,7 @@
                 b0_row.wait_recv()
                 remaining = jnp.concatenate([b0_all[s] for s in range(rows)], axis=1)
             else:
-                remaining = jnp.concatenate(
-                    [b1_all[s, t - 1] for s in range(rows)], axis=1
-                ) - own
+                remaining = -own
                 for peer in reversed(peers):
                     remote(
                         part_out.at[t], part_in.at[t, peer], part_sems.at[0, t, peer],
@@ -258,9 +340,10 @@
             sent = jnp.where(is_live, solved, 0.0).astype(jnp.bfloat16)
             sents.append(sent)
             if t + 1 < sections:
-                own = dot_nt(sent, panel(t + 1, t))
-                if older is not None:
-                    own = own + older
+                if t == 0:
+                    cross_wait.wait_recv()
+                    older = -placed(1)
+                own = dot_nt(sent, panel(t + 1, t)) + older
                 part_out[t + 1] = encode(own, SPARE)
                 for peer in peers:
                     copy = remote(
@@ -277,14 +360,12 @@
             copy.start()
             pending.append(copy)
             trail(t, sent)
-            if t == 0:
-                b1_row.wait_recv()
             if t + 2 < sections:
-                older = dot_nt(sents[0], panel(t + 2, 0))
-                for u in range(1, t + 1):
+                older = -placed(t + 2)
+                for u in range(t + 1):
                     older = older + dot_nt(sents[u], panel(t + 2, u))
 
-        for wait in (b0_wait, b1_wait, b0_row, b1_row):
+        for wait in (b0_wait, b0_row, line_wait, cross_wait):
             wait.wait_send()
         for copy in pairs + pending:
             copy.wait_send()
@@ -293,7 +374,7 @@
     totals = [acc[j] for j in range(rows_dev)]
     for s in range(rows):
         spans.append([x[:, s * width:(s + 1) * width] for x in totals])
-        tail_out[s] = encode(jnp.concatenate(spans[s], axis=1), SPARE)
+        tail_out[s] = jnp.concatenate(spans[s], axis=1).astype(jnp.bfloat16)
     tails = []
     for peer in peers:
         copy = remote(
@@ -313,7 +394,7 @@
             tail_out.at[peer], tail_in.at[peer], tail_sems.at[0, peer], tail_sems.at[1, peer],
             {"row": peer},
         ).wait_recv()
-        other = decode(tail_in[peer], rows_dev * width)
+        other = tail_in[peer].astype(jnp.float32)
         for j in range(rows_dev):
             values[j] = values[j] - other[:, j * width:(j + 1) * width]
     for j in range(rows_dev):
@@ -348,19 +429,24 @@
             [pltpu.VMEM((chips, tile // chips, width), bf16)] * count,
             pltpu.VMEM((count, tile // chips, width), bf16),
             [pltpu.VMEM((tile, width), bf16)] * count,
+            [pltpu.VMEM((SIDE, tile // SIDE, width), bf16)] * count,
+            [pltpu.VMEM((tile // SIDE, width), bf16)] * count,
+            [pltpu.VMEM((SIDE, tile // chips, width), bf16)] * count,
+            [pltpu.VMEM((tile // SIDE, width), bf16)] * count,
             pltpu.VMEM((sections, rhs_count, width), f32),
             pltpu.VMEM((sections, rhs_count, width), f32),
             pltpu.VMEM((sections, rhs_count, width), f32),
             pltpu.VMEM((chips, rhs_count, width), f32),
-            pltpu.VMEM((chips, sections - 1, rhs_count, width), f32),
             pltpu.VMEM((rows, rhs_count, width), f32),
-            pltpu.VMEM((rows, sections - 1, rhs_count, width), f32),
+            pltpu.VMEM((SIDE, sections - 1, rhs_count, width), f32),
+            pltpu.VMEM((sections - 1, rhs_count, width), f32),
+            pltpu.VMEM((SIDE, sections - 1, rhs_count, width), f32),
             pltpu.VMEM((sections, rhs_count, tile + SPARE), i16),
             pltpu.VMEM((sections, rows, rhs_count, tile + SPARE), i16),
             pltpu.VMEM((sections, rhs_count, width), f32),
             pltpu.VMEM((rows_dev, rhs_count, tile), f32),
-            pltpu.VMEM((rows, rhs_count, rows_dev * width + SPARE), i16),
-            pltpu.VMEM((rows, rhs_count, rows_dev * width + SPARE), i16),
+            pltpu.VMEM((rows, rhs_count, rows_dev * width), bf16),
+            pltpu.VMEM((rows, rhs_count, rows_dev * width), bf16),
             pltpu.VMEM(right_side.shape, f32),
             pltpu.SMEM(tile_order.shape, jnp.int32),
             pltpu.SMEM(live_segments.shape, jnp.int32),
@@ -371,6 +457,7 @@
             dma((2,)),
             dma((2, count)),
             dma((2, count)),
+            dma((3, 2, count)),
             dma((2, 2)),
             dma((2, 2)),
             dma((2, sections, rows)),

time: 65.6 us -> 61.8 us (0.942)
  Pallas kernels: 64.1 us -> 60.1 us
    pallas_call x1, Pallas kernels: 64.1 us -> 60.1 us  [per_device(): pl.pallas_call(functools.partial(kernel, rows, cols, blocks), out_shape=j...]
where the time goes in v2:
time: 61.8 us; the launch traced here: 61.4 us
  Pallas kernels  60.1 us (97%)
  local copies, waits for them, and re-layouts  1.38 us (2%)
    pallas_call x1, Pallas kernels, per_device(): pl.pallas_call(functools.partial(kernel, rows, cols, blocks), out_shape=j...  60.1 us
    unnamed x1, local copies, waits for them, and re-layouts  1.38 us

profile of v2, /device:TPU:1, one launch (start us, length us, event | category | flops | bytes accessed | tf_op | source)
XLA Modules:
  0.0 61.4 jit_solution(14756493468649373820)
XLA Ops:
  0.0 60.1 %shard_map.55 = f32[16,4,128]{2,1,0:T(4,128)} custom-call(bf16[5,4,1024,128]{3,2,1,0:T(8,128)(2,1)} %bitcast.3, bf16[5,128,1024]{2,1,0:T(8,128)(2,1)} %inverse_hbm.1, f32[16,4,128]{2,1,0:T(4,128)} %rhs_hbm.1, s32[128]{0:T(128)} %order_hbm.1, s32[16]{0:T(128)} %live_hbm.1), custom_call_target="tpu_custom_call" | custom-call | tf_op jit(solution)/shard_map/pallas_call | solution.py:419
  60.1 1.4 %copy.7 = f32[16,4,128]{2,1,0:T(4,128)} copy(f32[16,4,128]{2,1,0:T(4,128)} %shard_map.55) | data formatting | bytes 65536

commit v3 on v2

--- a/solution.py
+++ b/solution.py
@@ -9,8 +9,7 @@
 MESH = pl.DeviceIdType.MESH
 SPARE = 128
 SIDE = 4
-DIRECT = 10
-ORDER = "s0 s1 s2 s3 g0 s4 g1 s5 g2 s6 g3 s7 g4 s8 g5 s9 g6 g7 g8 g9"
+DEPTH = 4
 NT = (((1,), (1,)), ((), ()))
 
 
@@ -46,10 +45,10 @@
 
 def kernel(
     rows, cols, blocks, factor_hbm, inverse_hbm, rhs_hbm, order_hbm, live_hbm, out,
-    factor, inverse, cand, theirs, pieces, mine, panels, quarters, quarter, sixteenths, joined,
+    factor, inverse, cand, theirs, pieces, mine, panels,
     b_own, b_pair, b_chip, b0_in, b0_all, b_line, b_turn, b_cross,
     part_out, part_in, stored, acc, tail_out, tail_in, rhs, order, live,
-    factor_sem, inverse_sem, small_sem, pair_sems, b_sems, piece_sems, panel_sems, line_sems,
+    factor_sem, inverse_sem, small_sem, pair_sems, b_sems, piece_sems, panel_sems,
     b0_sems, b1_sems, part_sems, stored_sems, tail_sems,
 ):
     sections = len(factor)
@@ -153,73 +152,12 @@
                     panel_sems.at[0, i], panel_sems.at[1, i], {"col": 2 * p + 1},
                 ).start()
 
-        part = tile // SIDE
-        ahead = [d for d in ring_order(SIDE)]
-
-        def place(i):
-            t, u = blocks[i]
-            here = (lax.rem(chip, SIDE), lax.div(chip, SIDE))
-            root = (lax.rem(root_chip[t], SIDE), lax.div(root_chip[t], SIDE))
-            if i % 2:
-                here, root = here[::-1], root[::-1]
-                return here, root, lambda a, b: 2 * (a * SIDE + b)
-            return here, root, lambda a, b: 2 * (b * SIDE + a)
-
-        def line(i, stage, some):
-            return remote(
-                some, some, line_sems.at[stage, 0, i], line_sems.at[stage, 1, i], {"col": c + 1}
-            )
-
-        def first_line(i):
-            merge(i)
-            (a, b), root, core_of = place(i)
-            for d in ahead:
-                to = lax.rem(a + d, SIDE)
-                remote(
-                    cand[i].at[span(to, part)], quarters[i].at[a],
-                    line_sems.at[0, 0, i], line_sems.at[0, 1, i], {"col": core_of(to, b)},
-                ).start()
-            quarters[i][a] = cand[i][span(a, part)]
-
-        def second_line(i):
-            (a, b), root, core_of = place(i)
-            line(i, 0, quarters[i].at[pl.ds(0, SIDE - 1)]).wait_recv()
-            quarter[i][...] = quarters[i][root[0]]
-            for d in ahead:
-                to = lax.rem(b + d, SIDE)
-                remote(
-                    quarter[i].at[span(to, piece)], sixteenths[i].at[b],
-                    line_sems.at[1, 0, i], line_sems.at[1, 1, i], {"col": core_of(a, to)},
-                ).start()
-            sixteenths[i][b] = quarter[i][span(b, piece)]
-
-        def third_line(i):
-            (a, b), root, core_of = place(i)
-            line(i, 1, sixteenths[i].at[pl.ds(0, SIDE - 1)]).wait_recv()
-            joined[i][span(b, piece)] = sixteenths[i][root[1]]
-            for d in ahead:
-                remote(
-                    joined[i].at[span(b, piece)], joined[i].at[span(b, piece)],
-                    line_sems.at[2, 0, i], line_sems.at[2, 1, i],
-                    {"col": core_of(a, lax.rem(b + d, SIDE))},
-                ).start()
-
-        def fourth_line(i):
-            (a, b), root, core_of = place(i)
-            line(i, 2, joined[i].at[pl.ds(0, part - piece)]).wait_recv()
-            for d in ahead + [0]:
-                remote(
-                    joined[i], panels[i].at[span(a, part)],
-                    panel_sems.at[0, i], panel_sems.at[1, i],
-                    {"col": core_of(lax.rem(a + d, SIDE), b) + 1},
-                ).start()
-
-        direct = range(DIRECT)
-        run = dict(
-            s=scatter, g=gather, a=first_line, b=second_line, c=third_line, d=fourth_line
-        )
-        for op in ORDER.split():
-            run[op[0]](int(op[1:]))
+        for i in range(DEPTH):
+            scatter(i)
+        for i in range(len(blocks)):
+            gather(i)
+            if i + DEPTH < len(blocks):
+                scatter(i + DEPTH)
 
         for t in range(sections):
             remote(
@@ -230,15 +168,8 @@
 
         pair.wait_send()
         for i in range(len(blocks)):
-            if i in direct:
-                some = pieces[i].at[pl.ds(0, chips - 1)]
-                remote(
-                    some, some, piece_sems.at[0, i], piece_sems.at[1, i], {"col": c + 1}
-                ).wait_send()
-            else:
-                line(i, 0, quarters[i].at[pl.ds(0, SIDE - 1)]).wait_send()
-                line(i, 1, sixteenths[i].at[pl.ds(0, SIDE - 1)]).wait_send()
-                line(i, 2, joined[i].at[pl.ds(0, part - piece)]).wait_send()
+            some = pieces[i].at[pl.ds(0, chips - 1)]
+            remote(some, some, piece_sems.at[0, i], piece_sems.at[1, i], {"col": c + 1}).wait_send()
             remote(
                 panels[i], panels[i], panel_sems.at[0, i], panel_sems.at[1, i], {"col": c + 1}
             ).wait_send()
@@ -249,21 +180,6 @@
             for s in range(0, tile, 256):
                 cand[i][s:s + 256] = factor[u][locals_[t], pl.ds(s, 256), :]
         pl.semaphore_wait(barrier, rows - 1 + cols - 1)
-        remote(b_own, b_pair, b_sems.at[0], b_sems.at[1], {"col": c - 1}).wait_recv()
-        for t in range(sections):
-            b_chip[t] = jnp.where(root_core[t] == 1, b_own[t], b_pair[t])
-        for p in others:
-            remote(
-                b_chip.at[0], b0_in.at[chip], b0_sems.at[0, 0], b0_sems.at[1, 0],
-                {"col": 2 * p + 1},
-            ).start()
-        chip_y, chip_x = lax.div(chip, SIDE), lax.rem(chip, SIDE)
-        for d in ring_order(SIDE):
-            to = chip_y * SIDE + lax.rem(chip_x + d, SIDE)
-            remote(
-                b_chip.at[pl.ds(1, sections - 1)], b_line.at[chip_x],
-                b1_sems.at[0, 0], b1_sems.at[1, 0], {"col": 2 * to + 1},
-            ).start()
         pairs = []
         for i in range(len(blocks)):
             copy = remote(
@@ -271,6 +187,21 @@
             )
             copy.start()
             pairs.append(copy)
+        remote(b_own, b_pair, b_sems.at[0], b_sems.at[1], {"col": c - 1}).wait_recv()
+        for t in range(sections):
+            b_chip[t] = jnp.where(root_core[t] == 1, b_own[t], b_pair[t])
+        for p in others:
+            remote(
+                b_chip.at[0], b0_in.at[chip], b0_sems.at[0, 0], b0_sems.at[1, 0],
+                {"col": 2 * p + 1},
+            ).start()
+        chip_y, chip_x = lax.div(chip, SIDE), lax.rem(chip, SIDE)
+        for d in ring_order(SIDE):
+            to = chip_y * SIDE + lax.rem(chip_x + d, SIDE)
+            remote(
+                b_chip.at[pl.ds(1, sections - 1)], b_line.at[chip_x],
+                b1_sems.at[0, 0], b1_sems.at[1, 0], {"col": 2 * to + 1},
+            ).start()
         b0_in[chip] = b_chip[0]
         b_line[chip_x] = b_chip[1:]
 
@@ -429,10 +360,6 @@
             [pltpu.VMEM((chips, tile // chips, width), bf16)] * count,
             pltpu.VMEM((count, tile // chips, width), bf16),
             [pltpu.VMEM((tile, width), bf16)] * count,
-            [pltpu.VMEM((SIDE, tile // SIDE, width), bf16)] * count,
-            [pltpu.VMEM((tile // SIDE, width), bf16)] * count,
-            [pltpu.VMEM((SIDE, tile // chips, width), bf16)] * count,
-            [pltpu.VMEM((tile // SIDE, width), bf16)] * count,
             pltpu.VMEM((sections, rhs_count, width), f32),
             pltpu.VMEM((sections, rhs_count, width), f32),
             pltpu.VMEM((sections, rhs_count, width), f32),
@@ -457,7 +384,6 @@
             dma((2,)),
             dma((2, count)),
             dma((2, count)),
-            dma((3, 2, count)),
             dma((2, 2)),
             dma((2, 2)),
             dma((2, sections, rows)),

time: 61.8 us -> 60.1 us (0.972)
  Pallas kernels: 60.1 us -> 58.6 us
    pallas_call x1, Pallas kernels: 60.1 us -> 58.6 us  [per_device(): pl.pallas_call(functools.partial(kernel, rows, cols, blocks), out_shape=j...]
where the time goes in v3:
time: 60.1 us; the launch traced here: 60 us
  Pallas kernels  58.6 us (98%)
  local copies, waits for them, and re-layouts  1.38 us (2%)
    pallas_call x1, Pallas kernels, per_device(): pl.pallas_call(functools.partial(kernel, rows, cols, blocks), out_shape=j...  58.6 us
    unnamed x1, local copies, waits for them, and re-layouts  1.38 us

profile of v3, /device:TPU:1, one launch (start us, length us, event | category | flops | bytes accessed | tf_op | source)
XLA Modules:
  0.0 60.0 jit_solution(7235181230443169200)
XLA Ops:
  0.0 58.6 %shard_map.55 = f32[16,4,128]{2,1,0:T(4,128)} custom-call(bf16[5,4,1024,128]{3,2,1,0:T(8,128)(2,1)} %bitcast.3, bf16[5,128,1024]{2,1,0:T(8,128)(2,1)} %inverse_hbm.1, f32[16,4,128]{2,1,0:T(4,128)} %rhs_hbm.1, s32[128]{0:T(128)} %order_hbm.1, s32[16]{0:T(128)} %live_hbm.1), custom_call_target="tpu_custom_call" | custom-call | tf_op jit(solution)/shard_map/pallas_call | solution.py:350
  58.6 1.4 %copy.7 = f32[16,4,128]{2,1,0:T(4,128)} copy(f32[16,4,128]{2,1,0:T(4,128)} %shard_map.55) | data formatting | bytes 65536

commit v4 on v3

--- a/solution.py
+++ b/solution.py
@@ -47,9 +47,9 @@
     rows, cols, blocks, factor_hbm, inverse_hbm, rhs_hbm, order_hbm, live_hbm, out,
     factor, inverse, cand, theirs, pieces, mine, panels,
     b_own, b_pair, b_chip, b0_in, b0_all, b_line, b_turn, b_cross,
-    part_out, part_in, stored, acc, tail_out, tail_in, rhs, order, live,
+    part_out, part_in, stored, acc, tail_out, tail_in, mate_factor, mate_acc, mate_out, rhs, order, live,
     factor_sem, inverse_sem, small_sem, pair_sems, b_sems, piece_sems, panel_sems,
-    b0_sems, b1_sems, part_sems, stored_sems, tail_sems,
+    b0_sems, b1_sems, part_sems, stored_sems, tail_sems, mate_sems, mate_tail_sems,
 ):
     sections = len(factor)
     rows_dev, tile, width = factor[0].shape
@@ -82,6 +82,12 @@
                 barrier, inc=1, device_id={axis: lax.rem(me + d, count)}, device_id_type=MESH
             )
 
+    for d in range(1, rows):
+        pl.semaphore_signal(
+            barrier, inc=1, device_id={"row": lax.rem(r + d, rows), "col": c + 1 - 2 * core},
+            device_id_type=MESH,
+        )
+
     for copy in small:
         copy.wait()
     slots = [order[u] for u in range(sections)]
@@ -112,11 +118,33 @@
             else:
                 acc[j] += update
 
+    last = sections - 1
+
+    def split(totals, to):
+        for s in range(rows):
+            spans = [x[:, s * width:(s + 1) * width] for x in totals]
+            to[s] = jnp.concatenate(spans, axis=1).astype(jnp.bfloat16)
+
+    def subtract(values, s):
+        other = tail_in[s].astype(jnp.float32)
+        return [x - other[:, j * width:(j + 1) * width] for j, x in enumerate(values)]
+
+    def finish(values):
+        for j in range(rows_dev):
+            value = values[j]
+            for t in range(sections):
+                value = jnp.where(slots[t] == c * rows_dev + j, stored[t], value)
+            out[:, j, :] = value
+
     @pl.when(core == 0)
     def _():
-        pl.semaphore_wait(barrier, rows - 1 + cols - 1)
+        pl.semaphore_wait(barrier, 2 * (rows - 1) + cols - 1)
         pair = remote(b_own, b_pair, b_sems.at[0], b_sems.at[1], {"col": c + 1})
         pair.start()
+        mates = [
+            remote(a, b, mate_sems.at[0, n], mate_sems.at[1, n], {"col": c + 1})
+            for n, (a, b) in enumerate(((factor[last], mate_factor), (acc, mate_acc)))
+        ]
 
         def merge(i):
             t, u = blocks[i]
@@ -164,8 +192,23 @@
                 stored.at[t], stored.at[t], stored_sems.at[0, t], stored_sems.at[1, t],
                 {"col": c + 1},
             ).wait_recv()
-            trail(t, jnp.where(limit > t, stored[t], 0.0).astype(jnp.bfloat16))
-
+            if t == 1:
+                mates[0].start()
+            if t < last:
+                trail(t, jnp.where(limit > t, stored[t], 0.0).astype(jnp.bfloat16))
+            if t == last - 1:
+                mates[1].start()
+
+        values = [rhs[:, j, :] for j in range(rows_dev)]
+        for s in [r] + peers[::-1]:
+            remote(
+                tail_in.at[s], tail_in.at[s], mate_tail_sems.at[s], tail_sems.at[1, s],
+                {"col": c + 1},
+            ).wait_recv()
+            values = subtract(values, s)
+        finish(values)
+        for copy in mates:
+            copy.wait_send()
         pair.wait_send()
         for i in range(len(blocks)):
             some = pieces[i].at[pl.ds(0, chips - 1)]
@@ -179,7 +222,7 @@
         for i, (t, u) in enumerate(blocks):
             for s in range(0, tile, 256):
                 cand[i][s:s + 256] = factor[u][locals_[t], pl.ds(s, 256), :]
-        pl.semaphore_wait(barrier, rows - 1 + cols - 1)
+        pl.semaphore_wait(barrier, 2 * (rows - 1) + cols - 1)
         pairs = []
         for i in range(len(blocks)):
             copy = remote(
@@ -242,6 +285,10 @@
             ).wait_recv()
             return panels[i][...]
 
+        mates = [
+            remote(x, x, mate_sems.at[0, n], mate_sems.at[1, n], {"col": c - 1})
+            for n, x in enumerate((mate_factor, mate_acc))
+        ]
         sents, pending = [], []
         own, older = None, None
         for t in range(sections):
@@ -283,6 +330,35 @@
                     )
                     copy.start()
                     pending.append(copy)
+            if t == last:
+                for copy in mates:
+                    copy.wait_recv()
+                totals = [acc[j] + dot_nt(sent, factor[t][j]) for j in range(rows_dev)]
+                split(totals, tail_out)
+                for peer in peers:
+                    copy = remote(
+                        tail_out.at[peer], tail_in.at[r], tail_sems.at[0, peer],
+                        tail_sems.at[1, r], {"row": peer},
+                    )
+                    copy.start()
+                    pending.append(copy)
+                split(
+                    [mate_acc[j] + dot_nt(sent, mate_factor[j]) for j in range(rows_dev)],
+                    mate_out,
+                )
+                for peer in peers:
+                    copy = remote(
+                        mate_out.at[peer], tail_in.at[r], mate_tail_sems.at[peer],
+                        tail_sems.at[1, r], {"row": peer, "col": c - 1},
+                    )
+                    copy.start()
+                    pending.append(copy)
+                copy = remote(
+                    mate_out.at[r], tail_in.at[r], mate_tail_sems.at[r], tail_sems.at[1, r],
+                    {"col": c - 1},
+                )
+                copy.start()
+                pending.append(copy)
             stored[t] = jnp.where(is_live, solved, kept)
             copy = remote(
                 stored.at[t], stored.at[t], stored_sems.at[0, t], stored_sems.at[1, t],
@@ -290,51 +366,30 @@
             )
             copy.start()
             pending.append(copy)
-            trail(t, sent)
+            if t < last:
+                trail(t, sent)
             if t + 2 < sections:
                 older = -placed(t + 2)
                 for u in range(t + 1):
                     older = older + dot_nt(sents[u], panel(t + 2, u))
 
+        values = []
+        for j in range(rows_dev):
+            total = totals[j][:, :width]
+            for s in range(1, rows):
+                total = jnp.where(r == s, totals[j][:, s * width:(s + 1) * width], total)
+            values.append(rhs[:, j, :] - total)
+        for peer in reversed(peers):
+            remote(
+                tail_out.at[peer], tail_in.at[peer], tail_sems.at[0, peer],
+                tail_sems.at[1, peer], {"row": peer},
+            ).wait_recv()
+            values = subtract(values, peer)
+        finish(values)
         for wait in (b0_wait, b0_row, line_wait, cross_wait):
             wait.wait_send()
         for copy in pairs + pending:
             copy.wait_send()
-
-    spans = []
-    totals = [acc[j] for j in range(rows_dev)]
-    for s in range(rows):
-        spans.append([x[:, s * width:(s + 1) * width] for x in totals])
-        tail_out[s] = jnp.concatenate(spans[s], axis=1).astype(jnp.bfloat16)
-    tails = []
-    for peer in peers:
-        copy = remote(
-            tail_out.at[peer], tail_in.at[r], tail_sems.at[0, peer], tail_sems.at[1, r],
-            {"row": peer},
-        )
-        copy.start()
-        tails.append(copy)
-    values = []
-    for j in range(rows_dev):
-        total = spans[0][j]
-        for s in range(1, rows):
-            total = jnp.where(r == s, spans[s][j], total)
-        values.append(rhs[:, j, :] - total)
-    for peer in reversed(peers):
-        remote(
-            tail_out.at[peer], tail_in.at[peer], tail_sems.at[0, peer], tail_sems.at[1, peer],
-            {"row": peer},
-        ).wait_recv()
-        other = tail_in[peer].astype(jnp.float32)
-        for j in range(rows_dev):
-            values[j] = values[j] - other[:, j * width:(j + 1) * width]
-    for j in range(rows_dev):
-        value = values[j]
-        for t in range(sections):
-            value = jnp.where(slots[t] == c * rows_dev + j, stored[t], value)
-        out[:, j, :] = value
-    for copy in tails:
-        copy.wait_send()
 
 
 def per_device(rows, cols, factor, diag_inverse, right_side, tile_order, live_segments):
@@ -374,6 +429,9 @@
             pltpu.VMEM((rows_dev, rhs_count, tile), f32),
             pltpu.VMEM((rows, rhs_count, rows_dev * width), bf16),
             pltpu.VMEM((rows, rhs_count, rows_dev * width), bf16),
+            pltpu.VMEM((rows_dev, tile, width), bf16),
+            pltpu.VMEM((rows_dev, rhs_count, tile), f32),
+            pltpu.VMEM((rows, rhs_count, rows_dev * width), bf16),
             pltpu.VMEM(right_side.shape, f32),
             pltpu.SMEM(tile_order.shape, jnp.int32),
             pltpu.SMEM(live_segments.shape, jnp.int32),
@@ -389,6 +447,8 @@
             dma((2, sections, rows)),
             dma((2, sections)),
             dma((2, rows)),
+            dma((2, 2)),
+            dma((rows,)),
         ],
         compiler_params=pltpu.CompilerParams(
             collective_id=0, has_side_effects=True, vmem_limit_bytes=67043328

time: 60.1 us -> 59.8 us (level)
  no operation moved by 1% of the time
where the time goes in v4:
time: 59.8 us; the launch traced here: 59.6 us
  Pallas kernels  58.3 us (97%)
  local copies, waits for them, and re-layouts  1.38 us (2%)
    pallas_call x1, Pallas kernels, per_device(): pl.pallas_call(functools.partial(kernel, rows, cols, blocks), out_shape=j...  58.3 us
    unnamed x1, local copies, waits for them, and re-layouts  1.38 us

profile of v4, /device:TPU:1, one launch (start us, length us, event | category | flops | bytes accessed | tf_op | source)
XLA Modules:
  0.0 59.6 jit_solution(16872328832554299226)
XLA Ops:
  0.0 58.3 %shard_map.55 = f32[16,4,128]{2,1,0:T(4,128)} custom-call(bf16[5,4,1024,128]{3,2,1,0:T(8,128)(2,1)} %bitcast.3, bf16[5,128,1024]{2,1,0:T(8,128)(2,1)} %inverse_hbm.1, f32[16,4,128]{2,1,0:T(4,128)} %rhs_hbm.1, s32[128]{0:T(128)} %order_hbm.1, s32[16]{0:T(128)} %live_hbm.1), custom_call_target="tpu_custom_call" | custom-call | tf_op jit(solution)/shard_map/pallas_call | solution.py:405
  58.3 1.4 %copy.7 = f32[16,4,128]{2,1,0:T(4,128)} copy(f32[16,4,128]{2,1,0:T(4,128)} %shard_map.55) | data formatting | bytes 65536

commit v5 on v4

--- a/solution.py
+++ b/solution.py
@@ -60,6 +60,19 @@
     chip, core = lax.div(c, 2), lax.rem(c, 2)
     index = {tu: i for i, tu in enumerate(blocks)}
 
+    barrier = pltpu.get_barrier_semaphore()
+    for axis, me, count in (("row", r, rows), ("col", c, cols)):
+        for d in range(1, count):
+            pl.semaphore_signal(
+                barrier, inc=1, device_id={axis: lax.rem(me + d, count)}, device_id_type=MESH
+            )
+
+    for d in range(1, rows):
+        pl.semaphore_signal(
+            barrier, inc=1, device_id={"row": lax.rem(r + d, rows), "col": c + 1 - 2 * core},
+            device_id_type=MESH,
+        )
+
     small = (
         pltpu.make_async_copy(rhs_hbm, rhs, small_sem.at[0]),
         pltpu.make_async_copy(order_hbm, order, small_sem.at[1]),
@@ -74,19 +87,6 @@
         factor_loads.append(copy)
     inverse_load = pltpu.make_async_copy(inverse_hbm, inverse, inverse_sem.at[0])
     inverse_load.start()
-
-    barrier = pltpu.get_barrier_semaphore()
-    for axis, me, count in (("row", r, rows), ("col", c, cols)):
-        for d in range(1, count):
-            pl.semaphore_signal(
-                barrier, inc=1, device_id={axis: lax.rem(me + d, count)}, device_id_type=MESH
-            )
-
-    for d in range(1, rows):
-        pl.semaphore_signal(
-            barrier, inc=1, device_id={"row": lax.rem(r + d, rows), "col": c + 1 - 2 * core},
-            device_id_type=MESH,
-        )
 
     for copy in small:
         copy.wait()

time: 59.8 us -> 59.7 us (level)
  no operation moved by 1% of the time
where the time goes in v5:
time: 59.7 us; the launch traced here: 59.6 us
  Pallas kernels  58.2 us (97%)
  local copies, waits for them, and re-layouts  1.38 us (2%)
    pallas_call x1, Pallas kernels, per_device(): pl.pallas_call(functools.partial(kernel, rows, cols, blocks), out_shape=j...  58.2 us
    unnamed x1, local copies, waits for them, and re-layouts  1.38 us

profile of v5, /device:TPU:1, one launch (start us, length us, event | category | flops | bytes accessed | tf_op | source)
XLA Modules:
  0.0 59.6 jit_solution(3885981287270125937)
XLA Ops:
  0.0 58.2 %shard_map.55 = f32[16,4,128]{2,1,0:T(4,128)} custom-call(bf16[5,4,1024,128]{3,2,1,0:T(8,128)(2,1)} %bitcast.3, bf16[5,128,1024]{2,1,0:T(8,128)(2,1)} %inverse_hbm.1, f32[16,4,128]{2,1,0:T(4,128)} %rhs_hbm.1, s32[128]{0:T(128)} %order_hbm.1, s32[16]{0:T(128)} %live_hbm.1), custom_call_target="tpu_custom_call" | custom-call | tf_op jit(solution)/shard_map/pallas_call | solution.py:405
  58.2 1.4 %copy.7 = f32[16,4,128]{2,1,0:T(4,128)} copy(f32[16,4,128]{2,1,0:T(4,128)} %shard_map.55) | data formatting | bytes 65536
